TPU v7x, 32 devices: a whole 2x2x4 slice. The times are simulated.
32 devices in a mesh: section: 4 (over x, core), tensor: 2 (over y), dp: 4 (over z).
Axes of the slice: x: 2, y: 2, z: 4, core: 2. Of those that a mesh axis runs over, the one named last changes fastest.
Arguments:
- residuals: bfloat16 [4, 4, 2, 128, 8192], P('section', 'dp', None, 'tensor'), may hold values from -6 to 6
- norm_gain: bfloat16 [4, 8192], P('section'), may hold values from 0.5 to 1.5
- projection: bfloat16 [4, 8192, 2, 2, 128], P('section', None, 'tensor'), may hold values from -0.0625 to 0.0625
- queries: bfloat16 [4, 4, 2, 128, 2, 1024], P('section', 'dp', None, None, 'tensor'), may hold values from -48 to 48
- output_grad: bfloat16 [4, 4, 2, 128, 2, 1024], P('section', 'dp', None, None, 'tensor'), may hold values from -6 to 6
- section_cotangent: bfloat16 [4, 4, 128, 8192], P('section', 'dp', 'tensor'), may hold values from -6 to 6
- loss_cotangent: bfloat16 [4, 128, 8192], P('dp', 'tensor'), may hold values from -6 to 6
- lengths: int32 [4, 4, 2], P('section', 'dp'), may hold values from 64 to 128
- segments: int32 [4, 4, 2, 128], P('section', 'dp'), may hold values from 0 to 2, never falling along the last dimension, each value on 1 to 64 neighbouring positions
Outputs:
- query_grad: bfloat16 [4, 4, 2, 128, 2, 1024], P('section', 'dp', None, None, 'tensor')
- residual_grad: bfloat16 [4, 4, 128, 8192], P('section', 'dp', 'tensor')
- projection_grad: bfloat16 [4, 8192, 2, 2, 128], P('section', 'dp', 'tensor')
All inputs are finite; a program needn't handle non-finite values.
Results may differ from a plain program's by a relative error of at most 0.015.
Values may be sent and summed in bfloat16 or wider, within the bound.
A program may use at most 64 MiB of HBM per device.

v0:
```python
import functools

import jax
import jax.numpy as jnp
from jax import lax
from jax.experimental import pallas as pl
from jax.experimental.pallas import tpu as pltpu
from jax.sharding import PartitionSpec as P

EPSILON = 1e-05
MASKED = -1e30
ROWS = 16
NT = (((1,), (1,)), ((), ()))
TN = (((0,), (0,)), ((), ()))


def dot(left, right, dims=(((1,), (0,)), ((), ()))):
    return lax.dot_general(left, right, dims, preferred_element_type=jnp.float32)


def kernel(
    sizes,
    x_hbm, gain_ref, w_hbm, q_hbm, og_hbm, sc_hbm, lc_hbm, len_ref, seg_ref,
    qg_hbm, rg_hbm, pg_hbm,
    x, w, q, og, sc, lc, wo, nb, inv, cols, rows_in, part_out, part_in, proj,
    pair, pairs_in, back_out, back_in, feat_out, feat_in, feat_own, total,
    sum_own, sum_out, sum_in, outgoing, incoming, qg,
    local_sem, wo_s, wo_r, col_s, col_r, row_s, row_r, part_s, part_r, pair_s, pair_r,
    back_s, back_r, feat_s, feat_r, sum_s, sum_r, out_s, out_r,
):
    S, T, N, R, D, PW, G = sizes
    HS = PW // 2
    TOK, BW = R * T, D // N
    HB = BW // 2
    section, me_t, me_n = (lax.axis_index(name) for name in ("section", "tensor", "dp"))
    scaling = HS ** (-0.5)

    def peer(k, j):
        return {"tensor": lax.rem(me_t + k, T), "dp": lax.rem(me_n + j, N)}

    def block_at(j):
        return lax.rem(me_n + j, N)

    def remote(source, target, send, receive, device):
        return pltpu.make_async_remote_copy(
            src_ref=source, dst_ref=target, send_sem=send, recv_sem=receive,
            device_id=device, device_id_type=pl.DeviceIdType.MESH,
        )

    started = []

    def start(copies):
        for copy in copies:
            copy.start()
        started.extend(copies)
        return copies

    def arrive(copies):
        for copy in copies:
            copy.wait_recv()

    pairs_of = [(x_hbm.at[0], x.at[0]), (x_hbm.at[1], x.at[1]), (w_hbm, w), (q_hbm, q), (og_hbm, og),
                (sc_hbm, sc), (lc_hbm, lc)]
    loads = [pltpu.make_async_copy(a, b, local_sem.at[i]) for i, (a, b) in enumerate(pairs_of)]
    for load in loads:
        load.start()

    barrier = pltpu.get_barrier_semaphore()
    greet = [peer(k, j) for k in range(T) for j in range(N) if (k, j) != (0, 0)]
    down = {"section": lax.rem(section + S - 1, S)}
    greet = greet + [down, {"section": lax.rem(section + 1, S)}]
    for device in greet:
        pl.semaphore_signal(barrier, 1, device_id=device, device_id_type=pl.DeviceIdType.MESH)
    pl.semaphore_wait(barrier, len(greet))

    own_rows = pl.ds(pl.multiple_of(me_n * BW, BW), BW)
    weights_sent = start([
        remote(w_hbm.at[own_rows], wo.at[k - 1], wo_s.at[k - 1], wo_r.at[k - 1], peer(k, 0))
        for k in range(1, T)
    ])

    def normalize(tick):
        def step(i, _):
            rows = pl.ds(pl.multiple_of(i * ROWS, ROWS), ROWS)
            squares = jnp.zeros((ROWS, HB), jnp.float32)
            for p in range(2 * N):
                wide = x[tick, rows, p * HB:(p + 1) * HB].astype(jnp.float32)
                squares = squares + wide * wide
            inverse = lax.rsqrt(jnp.sum(squares, axis=1, keepdims=True) / D + EPSILON)
            inv[tick, rows, :] = inverse
            for p in range(2 * N):
                here = slice(p * HB, (p + 1) * HB)
                wide = x[tick, rows, here].astype(jnp.float32)
                gain = gain_ref[:, here].astype(jnp.float32)
                nb[tick, p // 2, p % 2, rows, :] = (wide * inverse * gain).astype(jnp.bfloat16)
            return _
        lax.fori_loop(0, R // ROWS, step, 0)
        for h in range(2):
            cols[tick, h, 0] = nb[tick, me_n, h]

    def send_columns(tick, h):
        return start([
            remote(nb.at[tick, block_at(j), h], cols.at[tick, h, j],
                   col_s.at[tick, h, j - 1], col_r.at[tick, h, j - 1], peer(0, j))
            for j in range(1, N)
        ])

    loads[0].wait()
    normalize(0)
    columns_sent = {(0, h): send_columns(0, h) for h in range(2)}
    loads[1].wait()
    normalize(1)
    loads[2].wait()

    own_tokens = pl.ds(pl.multiple_of(me_t * R, R), R)

    def tokens_of(k):
        return pl.ds(pl.multiple_of(lax.rem(me_t + k, T) * R, R), R)

    def project_own(tick):
        value = jnp.zeros((R, PW), jnp.float32)
        for p in range(2 * N):
            value = value + dot(nb[tick, p // 2, p % 2], w[p * HB:(p + 1) * HB, :])
        proj[own_tokens, :] = value.astype(jnp.bfloat16)

    def send_partials(tick, halves):
        sent = []
        for k in range(1, T):
            value = sum(
                dot(cols[tick, h].reshape(N * R, HB), wo[k - 1, h * HB:(h + 1) * HB, :]) for h in halves
            )
            part_out[tick, k - 1] = value.astype(jnp.bfloat16).reshape(N, R, PW)
            sent += [
                remote(part_out.at[tick, k - 1, j], part_in.at[tick, k - 1, j],
                       part_s.at[tick, k - 1, j], part_r.at[tick, k - 1, j], peer(T - k, N - j))
                for j in range(N)
            ]
        return start(sent)

    def gather_projected(tick, cross):
        project_own(tick)
        for k in range(1, T):
            value = jnp.sum(part_in[tick, k - 1].astype(jnp.float32), axis=0)
            if cross:
                for b in range(N):
                    value = value + dot(rows_in[T - k - 1, b], w[b * BW + HB:(b + 1) * BW, :])
            proj[tokens_of(k), :] = value.astype(jnp.bfloat16)

    position_q = lax.broadcasted_iota(jnp.int32, (TOK, TOK), 0)
    position_k = lax.broadcasted_iota(jnp.int32, (TOK, TOK), 1)

    def attend(tick):
        segment = jnp.broadcast_to(seg_ref[tick:tick + 1, :].astype(jnp.float32), (TOK, TOK))
        visible = (position_k <= position_q) & (segment == segment.T)
        live = lax.broadcasted_iota(jnp.int32, (TOK, HS), 0) < len_ref[tick]
        keys, values = proj[:, :HS], proj[:, HS:]
        key_grad = jnp.zeros((TOK, HS), jnp.float32)
        value_grad = jnp.zeros((TOK, HS), jnp.float32)
        for g in range(G):
            head = slice(g * HS, (g + 1) * HS)
            query = q[tick, :, head]
            masked = jnp.where(live, og[tick, :, head], jnp.zeros((), jnp.bfloat16))
            scores = jnp.where(visible, dot(query, keys, NT) * scaling, MASKED)
            exponent = jnp.exp(scores - jnp.max(scores, axis=1, keepdims=True))
            attention = exponent * (1.0 / jnp.sum(exponent, axis=1, keepdims=True))
            low = attention.astype(jnp.bfloat16)
            mixed = dot(low, values)
            correction = jnp.sum(mixed * masked.astype(jnp.float32), axis=1, keepdims=True)
            value_grad = value_grad + dot(low, masked, TN)
            weight_grad = dot(masked, values, NT)
            score_grad = (attention * (weight_grad - correction)).astype(jnp.bfloat16)
            qg[tick, :, head] = (dot(score_grad, keys) * scaling).astype(jnp.bfloat16)
            key_grad = key_grad + dot(score_grad, query, TN)
        pair[tick, :, :HS] = (key_grad * scaling).astype(jnp.bfloat16)
        pair[tick, :, HS:] = value_grad.astype(jnp.bfloat16)

    def send_pairs(tick):
        pairs_in[tick, 0, 0] = pair[tick, own_tokens, :]
        return start([
            remote(pair.at[tick, tokens_of(k)], pairs_in.at[tick, k, j],
                   pair_s.at[tick, k, j], pair_r.at[tick, k, j], peer(k, j))
            for j in range(N) for k in range(T) if (k, j) != (0, 0)
        ])

    def weights_of(k, columns):
        return w[pl.ds(pl.multiple_of(me_n * BW + columns.start, CH), columns.stop - columns.start), :] \
            if k == 0 else wo[k - 1, columns, :]

    CH = min(BW, 512)

    def send_back(tick, j):
        b = block_at(j)
        for c in range(0, BW, CH):
            rows = pl.ds(pl.multiple_of(b * BW + c, CH), CH)
            value = dot(pair[tick], w[rows, :], NT).astype(jnp.bfloat16)
            back_out[j - 1, :, :, c:c + CH] = value.reshape(T, R, CH)
        return start([
            remote(back_out.at[j - 1, lax.rem(me_t + k, T)], back_in.at[j - 1, k - 1],
                   back_s.at[j - 1, k - 1], back_r.at[j - 1, k - 1], peer(k, 0))
            for k in range(1, T)
        ])

    def own_feature_grad(tick):
        for c in range(0, BW, CH):
            here = slice(c, c + CH)
            value = jnp.zeros((R, CH), jnp.float32)
            for k in range(T):
                weights = weights_of(k, here)
                term = dot(pairs_in[tick, k, 0], weights, NT)
                value = value + term.astype(jnp.bfloat16).astype(jnp.float32)
            feat_own[:, here] = value

    def send_features(tick):
        sent = []
        for c in range(0, BW, CH):
            here = slice(c, c + CH)
            value = jnp.zeros((N * R, CH), jnp.float32)
            for k in range(T):
                term = dot(pairs_in[tick, k].reshape(N * R, PW), weights_of(k, here), NT)
                value = value + term.astype(jnp.bfloat16).astype(jnp.float32)
            feat_own[:, here] = value[:R]
            feat_out[:, :, here] = value[R:].astype(jnp.bfloat16).reshape(N - 1, R, CH)
        return start([
            remote(feat_out.at[j - 1], feat_in.at[j - 1], feat_s.at[j - 1], feat_r.at[j - 1], peer(0, N - j))
            for j in range(1, N)
        ])

    def norm_back(tick, base, target):
        def step(i, _):
            rows = pl.ds(pl.multiple_of(i * ROWS, ROWS), ROWS)
            inverse = inv[tick, rows, :]
            products = jnp.zeros((ROWS, BW), jnp.float32)
            for b in range(N):
                here = slice(b * BW, (b + 1) * BW)
                scaled = total[b, rows, :] * gain_ref[:, here].astype(jnp.float32)
                products = products + scaled * x[tick, rows, here].astype(jnp.float32)
            mean = jnp.sum(products, axis=1, keepdims=True) / D
            cube = inverse * inverse * inverse * mean
            for b in range(N):
                here = slice(b * BW, (b + 1) * BW)
                scaled = total[b, rows, :] * gain_ref[:, here].astype(jnp.float32)
                back = inverse * scaled - x[tick, rows, here].astype(jnp.float32) * cube
                target[rows, here] = (base(rows, here) + back).astype(jnp.bfloat16)
            return _
        lax.fori_loop(0, R // ROWS, step, 0)

    def accumulate(tick, k, first):
        right = pairs_in[tick, k].reshape(N * R, PW)
        for h in range(2):
            value = dot(cols[tick, h].reshape(N * R, HB), right, TN)
            here = slice(h * HB, (h + 1) * HB)
            sum_own[k, here, :] = value if first else sum_own[k, here, :] + value

    arrive(weights_sent)
    arrive(columns_sent[0, 0])
    arrive(columns_sent[0, 1])
    partials = [send_partials(0, (0, 1))]
    columns_sent[1, 0] = send_columns(1, 0)
    rows_sent = start([
        remote(nb.at[1, :, 1], rows_in.at[k - 1], row_s.at[k - 1], row_r.at[k - 1], peer(k, 0))
        for k in range(1, T)
    ])
    loads[3].wait()
    loads[4].wait()
    arrive(partials[0])
    gather_projected(0, False)
    attend(0)
    pairs_sent = [send_pairs(0)]

    arrive(columns_sent[1, 0])
    partials.append(send_partials(1, (0,)))
    columns_sent[1, 1] = send_columns(1, 1)
    backs_sent = [send_back(0, j) for j in range(1, N - 1)]
    arrive(pairs_sent[0])
    own_feature_grad(0)
    for k in range(T):
        accumulate(0, k, True)
    arrive(rows_sent)
    arrive(partials[1])
    gather_projected(1, True)
    attend(1)
    pairs_sent.append(send_pairs(1))
    backs_sent.append(send_back(0, N - 1))
    query_out = pltpu.make_async_copy(qg, qg_hbm, local_sem.at[3])
    query_out.start()

    arrive(pairs_sent[1])
    total[me_n] = feat_own[...]
    features_sent = send_features(1)
    arrive(columns_sent[1, 1])
    sums_sent = []
    for k in range(1, T):
        accumulate(1, k, False)
        sum_out[k - 1] = sum_own[k].astype(jnp.bfloat16)
        sums_sent += start([
            remote(sum_out.at[k - 1], sum_in.at[k - 1], sum_s.at[k - 1], sum_r.at[k - 1], peer(T - k, 0))
        ])
    accumulate(1, 0, False)

    for j in range(1, N):
        arrive(backs_sent[j - 1])
        value = back_out[j - 1, me_t].astype(jnp.float32)
        for k in range(1, T):
            value = value + back_in[j - 1, k - 1].astype(jnp.float32)
        total[block_at(j)] = value
    loads[5].wait()
    loads[6].wait()
    norm_back(0, lambda rows, here: sc[rows, here].astype(jnp.float32), outgoing)
    shift = start([remote(outgoing, incoming, out_s.at[0], out_r.at[0], down)])

    total[me_n] = feat_own[...]
    for j in range(1, N):
        arrive([features_sent[j - 1]])
        total[block_at(j)] = feat_in[j - 1].astype(jnp.float32)
    arrive(shift)
    is_last = section == S - 1

    def arriving(rows, here):
        return jnp.where(is_last, lc[rows, here].astype(jnp.float32), incoming[rows, here].astype(jnp.float32))

    for copy in shift:
        copy.wait_send()
    norm_back(1, arriving, outgoing)
    residual_out = pltpu.make_async_copy(outgoing, rg_hbm, local_sem.at[0])
    residual_out.start()

    for copy in sums_sent:
        copy.wait()
    final = sum_own[0]
    for k in range(1, T):
        final = final + sum_in[k - 1].astype(jnp.float32)
    sum_out[0] = final.astype(jnp.bfloat16)
    weight_out = pltpu.make_async_copy(sum_out.at[0], pg_hbm, local_sem.at[1])
    weight_out.start()
    for copy in started:
        if not any(copy is other for other in shift + sums_sent):
            copy.wait_send()
    query_out.wait()
    residual_out.wait()
    weight_out.wait()


def on_device(residuals, norm_gain, projection, queries, output_grad, section_cotangent, loss_cotangent, lengths, segments):
    x, q, og = residuals[0, 0], queries[0, 0, :, :, 0, :], output_grad[0, 0, :, :, 0, :]
    ticks, R, D = x.shape
    PW = 2 * projection.shape[4]
    S, T, N = (lax.axis_size(name) for name in ("section", "tensor", "dp"))
    TOK, BW, HB = R * T, D // N, D // N // 2
    sizes = (S, T, N, R, D, PW, q.shape[-1] // (PW // 2))
    low, wide, dma = jnp.bfloat16, jnp.float32, pltpu.SemaphoreType.DMA
    anywhere, vmem = pl.BlockSpec(memory_space=pl.ANY), pl.BlockSpec(memory_space=pltpu.VMEM)
    outs = pl.pallas_call(
        functools.partial(kernel, sizes),
        out_shape=(
            jax.ShapeDtypeStruct(q.shape, low),
            jax.ShapeDtypeStruct((R, D), low),
            jax.ShapeDtypeStruct((BW, PW), low),
        ),
        in_specs=[anywhere, vmem] + [anywhere] * 5 + [pl.BlockSpec(memory_space=pltpu.SMEM), vmem],
        out_specs=[anywhere] * 3,
        scratch_shapes=[
            pltpu.VMEM(x.shape, low), pltpu.VMEM((D, PW), low), pltpu.VMEM(q.shape, low), pltpu.VMEM(q.shape, low),
            pltpu.VMEM((R, D), low), pltpu.VMEM((R, D), low),
            pltpu.VMEM((T - 1, BW, PW), low),
            pltpu.VMEM((ticks, N, 2, R, HB), low), pltpu.VMEM((ticks, R, 1), wide),
            pltpu.VMEM((ticks, 2, N, R, HB), low), pltpu.VMEM((T - 1, N, R, HB), low),
            pltpu.VMEM((ticks, T - 1, N, R, PW), low), pltpu.VMEM((ticks, T - 1, N, R, PW), low),
            pltpu.VMEM((TOK, PW), low),
            pltpu.VMEM((ticks, TOK, PW), low), pltpu.VMEM((ticks, T, N, R, PW), low),
            pltpu.VMEM((N - 1, T, R, BW), low), pltpu.VMEM((N - 1, T - 1, R, BW), low),
            pltpu.VMEM((N - 1, R, BW), low), pltpu.VMEM((N - 1, R, BW), low), pltpu.VMEM((R, BW), wide),
            pltpu.VMEM((N, R, BW), wide),
            pltpu.VMEM((T, BW, PW), wide), pltpu.VMEM((T - 1, BW, PW), low), pltpu.VMEM((T - 1, BW, PW), low),
            pltpu.VMEM((R, D), low), pltpu.VMEM((R, D), low), pltpu.VMEM(q.shape, low),
            dma((7,)), dma((T - 1,)), dma((T - 1,)),
            dma((ticks, 2, N - 1)), dma((ticks, 2, N - 1)), dma((T - 1,)), dma((T - 1,)),
            dma((ticks, T - 1, N)), dma((ticks, T - 1, N)), dma((ticks, T, N)), dma((ticks, T, N)),
            dma((N - 1, T - 1)), dma((N - 1, T - 1)), dma((N - 1,)), dma((N - 1,)),
            dma((T - 1,)), dma((T - 1,)), dma((1,)), dma((1,)),
        ],
        compiler_params=pltpu.CompilerParams(
            collective_id=0, has_side_effects=True, vmem_limit_bytes=62_000_000
        ),
    )(
        x, norm_gain, projection.reshape(D, PW), q, og, section_cotangent[0, 0], loss_cotangent[0],
        lengths.reshape(ticks), segments[0, 0],
    )
    query_grad, residual_grad, projection_grad = outs
    return (
        query_grad[None, None, :, :, None, :],
        residual_grad[None, None],
        projection_grad.reshape(1, BW, 1, 2, PW // 2),
    )


def solution(mesh):
    in_specs = (
        P("section", "dp", None, "tensor", None),
        P("section", None),
        P("section", None, "tensor", None, None),
        P("section", "dp", None, None, "tensor", None),
        P("section", "dp", None, None, "tensor", None),
        P("section", "dp", "tensor", None),
        P("dp", "tensor", None),
        P("section", "dp", None),
        P("section", "dp", None, None),
    )
    out_specs = (
        P("section", "dp", None, None, "tensor", None),
        P("section", "dp", "tensor", None),
        P("section", "dp", "tensor", None, None),
    )
    return jax.shard_map(on_device, mesh=mesh, in_specs=in_specs, out_specs=out_specs, check_vma=False)
```

profile of v0, /device:TPU:0, one launch (start us, length us, event | category | flops | bytes accessed | tf_op | source)
XLA Modules:
  0.0 111.8 jit_solution(4017347934278274845)
XLA Ops:
  0.6 4.7 %copy.16 = bf16[1024,8,2,128]{3,1,2,0:T(8,128)(2,1)} copy(bf16[1024,8,2,128]{3,2,1,0:T(2,128)(2,1)} %bitcast.18) | data formatting | bytes 8388608
  5.3 100.2 %shard_map.112 = (bf16[2,128,1024]{2,1,0:T(8,128)(2,1)}, bf16[64,8192]{1,0:T(8,128)(2,1)}, bf16[2048,256]{1,0:T(8,128)(2,1)}) custom-call(bf16[2,64,8192]{2,1,0:T(8,128)(2,1)} %bitcast.19, bf16[1,8192]{1,0:T(2,128)(2,1)} %gain_ref.1, bf16[8192,256]{1,0:T(8,128)(2,1)} %bitcast.17, bf16[2,128,1024]{2,1,0:T(8,128)(2,1)} %bitcast.24, ...), custom_call_target="tpu_custom_call" | custom-call | tf_op jit(solution)/shard_map/pallas_call | solution.py:352
  105.5 2.1 %reshape.17 = bf16[1,2048,1,2,128]{4,3,1,2,0:T(2,128)(2,1)} reshape(bf16[2048,256]{1,0:T(8,128)(2,1)} %get-tuple-element.8) | data formatting | bytes 2097152 | tf_op jit(solution)/shard_map/reshape | solution.py:392
  107.6 1.9 %copy.19 = bf16[1,1,2,128,1,1024]{5,3,4,2,1,0:T(8,128)(2,1)} copy(bf16[1,1,2,128,1,1024]{5,3,4,2,1,0:T(8,128)(2,1)} %bitcast.26) | data formatting | bytes 1048576
  109.5 2.3 %copy.20 = bf16[1,1,64,8192]{3,2,1,0:T(8,128)(2,1)} copy(bf16[1,1,64,8192]{3,2,1,0:T(8,128)(2,1)} %bitcast.23) | data formatting | bytes 2097152
where the time goes:
time: 112 us
  Pallas kernels  100 us (89%)
  local copies, waits for them, and re-layouts  10.9 us (10%)
    pallas_call x1, Pallas kernels, on_device(): pl.pallas_call(functools.partial(kernel, sizes), out_shape=(jax.ShapeDtyp...  100 us
    unnamed x3, local copies, waits for them, and re-layouts  8.8 us

commit v1 on v0

v1 whole, which is shorter than its diff:
```python
import functools

import jax
import jax.numpy as jnp
from jax import lax
from jax.experimental import pallas as pl
from jax.experimental.pallas import tpu as pltpu
from jax.sharding import PartitionSpec as P

EPSILON = 1e-05
MASKED = -1e30
ROWS = 16
NT = (((1,), (1,)), ((), ()))
TN = (((0,), (0,)), ((), ()))


def dot(left, right, dims=(((1,), (0,)), ((), ()))):
    return lax.dot_general(left, right, dims, preferred_element_type=jnp.float32)


def kernel(
    sizes,
    x_hbm, gain_ref, w_hbm, q_hbm, og_hbm, sc_hbm, lc_hbm, len_ref, seg_ref,
    qg_hbm, rg_hbm, pg_hbm,
    x, raw, w, q, og, sc, lc, wo, nb, inv, cols, rows_in, part_out, part_in, part_sum, part_all, proj,
    pair, pairs_in, back_out, back_in, feat_out, feat_in, feat_own, total,
    sum_own, sum_out, sum_in, outgoing, incoming, result, qg, pg, stacked, score_grads,
    local_sem, raw_sem, wo_s, wo_r, col_s, col_r, row_s, row_r, part_s, part_r, psum_s, psum_r,
    pair_s, pair_r, pair_fs, pair_fr, back_s, back_r, feat_s, feat_r, sum_s, sum_r, out_s, out_r,
):
    S, T, N, R, D, PW, G = sizes
    HS = PW // 2
    TOK, BW = R * T, D // N
    HB = BW // 2
    WR = min(BW, 256)
    section, me_t, me_n = (lax.axis_index(name) for name in ("section", "tensor", "dp"))
    scaling = HS ** (-0.5)

    paired = N & (N - 1) == 0

    def block_at(j):
        if not paired:
            return lax.rem(me_n + j, N)
        at = me_n
        for bit in range(j.bit_length()):
            if j >> bit & 1:
                at = at + (1 << bit) * (1 - 2 * lax.rem(lax.div(me_n, 1 << bit), 2))
        return at

    def peer(k, j):
        return {"tensor": lax.rem(me_t + k, T), "dp": block_at(j)}

    def reverse(j):
        return j if paired else (N - j) % N

    def remote(source, target, send, receive, device):
        return pltpu.make_async_remote_copy(
            src_ref=source, dst_ref=target, send_sem=send, recv_sem=receive,
            device_id=device, device_id_type=pl.DeviceIdType.MESH,
        )

    started = []

    def start(copies):
        for copy in copies:
            copy.start()
        started.extend(copies)
        return copies

    def arrive(copies):
        for copy in copies:
            copy.wait_recv()

    own_rows = pl.ds(pl.multiple_of(me_n * BW, BW), BW)

    def weight_rows(j):
        return pl.ds(pl.multiple_of(block_at(j) * BW, BW), BW)

    raw_loads = [
        pltpu.make_async_copy(w_hbm.at[weight_rows(j)], raw.at[weight_rows(j)], raw_sem.at[j]) for j in range(N)
    ]
    pairs_of = [(x_hbm.at[0], x.at[0]), (x_hbm.at[1], x.at[1]), (q_hbm, q), (og_hbm, og), (sc_hbm, sc), (lc_hbm, lc)]
    loads = [pltpu.make_async_copy(a, b, local_sem.at[i]) for i, (a, b) in enumerate(pairs_of)]
    for load in loads[:1] + raw_loads[:1] + loads[1:2] + raw_loads[1:] + loads[2:]:
        load.start()

    barrier = pltpu.get_barrier_semaphore()
    greet = [peer(k, 0) for k in range(1, T)] + [peer(0, j) for j in range(1, N)]
    down = {"section": lax.rem(section + S - 1, S)}
    greet = greet + [down, {"section": lax.rem(section + 1, S)}]
    for device in greet:
        pl.semaphore_signal(barrier, 1, device_id=device, device_id_type=pl.DeviceIdType.MESH)

    def place_weights(j):
        raw_loads[j].wait()
        first = block_at(j) * BW

        def step(i, _):
            rows = pl.ds(pl.multiple_of(first + i * WR, WR), WR)
            w[rows, :] = raw[rows].reshape(WR, PW)
            return _
        lax.fori_loop(0, BW // WR, step, 0)

    def normalize(tick):
        def step(i, _):
            rows = pl.ds(pl.multiple_of(i * ROWS, ROWS), ROWS)
            squares = jnp.zeros((ROWS, HB), jnp.float32)
            for p in range(2 * N):
                wide = x[tick, rows, p * HB:(p + 1) * HB].astype(jnp.float32)
                squares = squares + wide * wide
            inverse = lax.rsqrt(jnp.sum(squares, axis=1, keepdims=True) / D + EPSILON)
            inv[tick, rows, :] = inverse
            for p in range(2 * N):
                here = slice(p * HB, (p + 1) * HB)
                wide = x[tick, rows, here].astype(jnp.float32)
                gain = gain_ref[:, here].astype(jnp.float32)
                nb[tick, p // 2, p % 2, rows, :] = (wide * inverse * gain).astype(jnp.bfloat16)
            return _
        lax.fori_loop(0, R // ROWS, step, 0)
        for h in range(2):
            cols[tick, h, 0] = nb[tick, me_n, h]

    def send_columns(tick, h, offsets=range(1, N)):
        return start([
            remote(nb.at[tick, block_at(j), h], cols.at[tick, h, j],
                   col_s.at[tick, h, j - 1], col_r.at[tick, h, j - 1], peer(0, j))
            for j in offsets
        ])

    own_tokens = pl.ds(pl.multiple_of(me_t * R, R), R)

    def tokens_of(k):
        return pl.ds(pl.multiple_of(lax.rem(me_t + k, T) * R, R), R)

    def project_own(tick):
        value = jnp.zeros((R, PW), jnp.float32)
        for p in range(2 * N):
            value = value + dot(nb[tick, p // 2, p % 2], w[p * HB:(p + 1) * HB, :])
        proj[tick, own_tokens, :] = value.astype(jnp.bfloat16)

    def send_partials(tick, halves):
        for k in range(1, T):
            value = sum(
                dot(cols[tick, h].reshape(N * R, HB), wo[k - 1, h * HB:(h + 1) * HB, :]) for h in halves
            )
            part_out[tick, :, k - 1] = value.astype(jnp.bfloat16).reshape(N, R, PW)
        return start([
            remote(part_out.at[tick, j], part_in.at[tick, j - 1],
                   part_s.at[tick, j - 1], part_r.at[tick, j - 1], peer(0, reverse(j)))
            for j in range(1, N)
        ])

    def send_part_sums(tick):
        value = part_out[tick, 0].astype(jnp.float32)
        for j in range(1, N):
            value = value + part_in[tick, j - 1].astype(jnp.float32)
        part_sum[tick] = value.astype(jnp.bfloat16)
        return start([
            remote(part_sum.at[tick, k - 1], part_all.at[tick, k - 1],
                   psum_s.at[tick, k - 1], psum_r.at[tick, k - 1], peer(T - k, 0))
            for k in range(1, T)
        ])

    def send_rows(piece):
        blocks = pl.ds(piece * (N // 2), N // 2)
        return start([
            remote(nb.at[1, blocks, 1], rows_in.at[k - 1, blocks], row_s.at[k - 1, piece], row_r.at[k - 1, piece], peer(k, 0))
            for k in range(1, T)
        ])

    def gather_projected(tick, cross):
        for k in range(1, T):
            value = part_all[tick, k - 1].astype(jnp.float32)
            if cross:
                for b in range(N):
                    value = value + dot(rows_in[T - k - 1, b], w[b * BW + HB:(b + 1) * BW, :])
            proj[tick, tokens_of(k), :] = value.astype(jnp.bfloat16)

    position_q = lax.broadcasted_iota(jnp.int32, (TOK, TOK), 0)
    position_k = lax.broadcasted_iota(jnp.int32, (TOK, TOK), 1)

    def stack_heads(tick):
        live = lax.broadcasted_iota(jnp.int32, (TOK, HS), 0) < len_ref[tick]
        for g in range(G):
            rows, head = slice(g * TOK, (g + 1) * TOK), slice(g * HS, (g + 1) * HS)
            stacked[tick, 0, rows, :] = q[tick, :, head]
            stacked[tick, 1, rows, :] = jnp.where(live, og[tick, :, head], jnp.zeros((), jnp.bfloat16))

    def attend(tick):
        segment = jnp.broadcast_to(seg_ref[tick:tick + 1, :].astype(jnp.float32), (TOK, TOK))
        visible = (position_k <= position_q) & (segment == segment.T)
        keys, values = proj[tick, :, :HS], proj[tick, :, HS:]
        query, masked = stacked[tick, 0], stacked[tick, 1]
        scores = (dot(query, keys, NT) * scaling).reshape(G, TOK, TOK)
        scores = jnp.where(visible[None], scores, MASKED)
        weight_grad = dot(masked, values, NT).reshape(G, TOK, TOK)
        exponent = jnp.exp(scores - jnp.max(scores, axis=2, keepdims=True))
        attention = exponent * (1.0 / jnp.sum(exponent, axis=2, keepdims=True))
        low = attention.astype(jnp.bfloat16).reshape(G * TOK, TOK)
        mixed = dot(low, values)
        correction = jnp.sum(mixed * masked.astype(jnp.float32), axis=1, keepdims=True).reshape(G, TOK, 1)
        score_grad = (attention * (weight_grad - correction)).astype(jnp.bfloat16).reshape(G * TOK, TOK)
        pair[tick, :, HS:] = dot(low, masked, TN).astype(jnp.bfloat16)
        pair[tick, :, :HS] = (dot(score_grad, query, TN) * scaling).astype(jnp.bfloat16)
        score_grads[tick] = score_grad

    def finish_queries(tick):
        value = (dot(score_grads[tick], proj[tick, :, :HS]) * scaling).astype(jnp.bfloat16)
        for g in range(G):
            qg[tick, :, g * HS:(g + 1) * HS] = value[g * TOK:(g + 1) * TOK]

    def send_pairs(tick):
        pairs_in[tick, 0, 0] = pair[tick, own_tokens, :]
        return start([
            remote(pair.at[tick, tokens_of(k)], pairs_in.at[tick, 0, k],
                   pair_s.at[tick, k - 1], pair_r.at[tick, k - 1], peer(k, 0))
            for k in range(1, T)
        ])

    def forward_pairs(ticks, heads, slot, offsets=range(1, N)):
        return {
            j: start([
                remote(pairs_in.at[ticks, 0, heads], pairs_in.at[ticks, j, heads],
                       pair_fs.at[slot, j - 1], pair_fr.at[slot, j - 1], peer(0, j))
            ])
            for j in offsets
        }

    def pairs_of_head(tick, k):
        return pairs_in[tick, :, k].reshape(N * R, PW)

    def weights_of(k, columns):
        return w[pl.ds(pl.multiple_of(me_n * BW + columns.start, CH), columns.stop - columns.start), :] \
            if k == 0 else wo[k - 1, columns, :]

    CH = min(BW, 512)

    def send_back(tick, j):
        b = block_at(j)
        for c in range(0, BW, CH):
            rows = pl.ds(pl.multiple_of(b * BW + c, CH), CH)
            value = dot(pair[tick], w[rows, :], NT).astype(jnp.bfloat16)
            back_out[tick, j - 1, :, :, c:c + CH] = value.reshape(T, R, CH)
        return start([
            remote(back_out.at[tick, j - 1, lax.rem(me_t + k, T)], back_in.at[tick, j - 1, k - 1],
                   back_s.at[tick, j - 1, k - 1], back_r.at[tick, j - 1, k - 1], peer(k, 0))
            for k in range(1, T)
        ])

    def feature_grads(tick, slots):
        for c in range(0, BW, CH):
            here = slice(c, c + CH)
            value = jnp.zeros((slots * R, CH), jnp.float32)
            for k in range(T):
                pairs = pairs_in[tick, :slots, k].reshape(slots * R, PW)
                term = dot(pairs, weights_of(k, here), NT)
                value = value + term.astype(jnp.bfloat16).astype(jnp.float32)
            feat_own[tick, :, here] = value[:R]
            feat_out[tick, :slots - 1, :, here] = value[R:].astype(jnp.bfloat16).reshape(slots - 1, R, CH)

    def send_features(tick, offsets):
        return {
            j: start([
                remote(feat_out.at[tick, j - 1], feat_in.at[tick, j - 1],
                       feat_s.at[tick, j - 1], feat_r.at[tick, j - 1], peer(0, reverse(j)))
            ])
            for j in offsets
        }

    def collect(tick, backs, features):
        total[me_n] = feat_own[tick]
        for j in backs:
            arrive(backs[j])
            value = back_out[tick, j - 1, me_t].astype(jnp.float32)
            for k in range(1, T):
                value = value + back_in[tick, j - 1, k - 1].astype(jnp.float32)
            total[block_at(j)] = value
        for j in features:
            arrive(features[j])
            total[block_at(j)] = feat_in[tick, j - 1].astype(jnp.float32)

    def norm_back(tick, base, target):
        def step(i, _):
            rows = pl.ds(pl.multiple_of(i * ROWS, ROWS), ROWS)
            inverse = inv[tick, rows, :]
            products = jnp.zeros((ROWS, BW), jnp.float32)
            for b in range(N):
                here = slice(b * BW, (b + 1) * BW)
                scaled = total[b, rows, :] * gain_ref[:, here].astype(jnp.float32)
                products = products + scaled * x[tick, rows, here].astype(jnp.float32)
            mean = jnp.sum(products, axis=1, keepdims=True) / D
            cube = inverse * inverse * inverse * mean
            for b in range(N):
                here = slice(b * BW, (b + 1) * BW)
                scaled = total[b, rows, :] * gain_ref[:, here].astype(jnp.float32)
                back = inverse * scaled - x[tick, rows, here].astype(jnp.float32) * cube
                target[rows, here] = (base(rows, here) + back).astype(jnp.bfloat16)
            return _
        lax.fori_loop(0, R // ROWS, step, 0)

    def accumulate(k, h):
        here = slice(h * HB, (h + 1) * HB)
        value = sum(dot(cols[tick, h].reshape(N * R, HB), pairs_of_head(tick, k), TN) for tick in range(2))
        if k == 0:
            sum_own[here, :] = value
        else:
            sum_out[k - 1, here, :] = value.astype(jnp.bfloat16)

    by_tensor = [list(range(2, N)), [N // 2]]
    by_dp = [[j for j in range(1, N) if j not in by_tensor[tick]] for tick in range(2)]

    loads[0].wait()
    normalize(0)
    pl.semaphore_wait(barrier, len(greet))
    columns_sent = {(0, h): send_columns(0, h) for h in range(2)}
    place_weights(0)
    weights_sent = start([
        remote(w.at[own_rows], wo.at[k - 1], wo_s.at[k - 1], wo_r.at[k - 1], peer(k, 0)) for k in range(1, T)
    ])
    loads[1].wait()
    normalize(1)
    rows_sent = send_rows(0)
    for j in range(1, N):
        place_weights(j)
    for tick in range(2):
        project_own(tick)
    for load in loads[2:4]:
        load.wait()
    for tick in range(2):
        stack_heads(tick)

    arrive(weights_sent)
    arrive(columns_sent[0, 0])
    arrive(columns_sent[0, 1])
    near, far = range(1, 2), range(2, N)
    partials = send_partials(0, (0, 1))
    columns_sent[1, 0] = send_columns(1, 0, near)
    columns_sent[1, 0] = columns_sent[1, 0] + send_columns(1, 0, far)
    arrive(partials)
    part_sums = [send_part_sums(0)]
    rows_sent = rows_sent + send_rows(1)
    arrive(part_sums[0])
    gather_projected(0, False)
    attend(0)
    pairs_sent = send_pairs(0)
    backs = [{}, {}]
    first, *rest = by_tensor[0]
    backs[0][first] = send_back(0, first)
    arrive(columns_sent[1, 0])
    partials = send_partials(1, (0,))
    columns_sent[1, 1] = send_columns(1, 1, near)
    columns_sent[1, 1] = columns_sent[1, 1] + send_columns(1, 1, far)
    finish_queries(0)
    arrive(partials)
    part_sums.append(send_part_sums(1))
    arrive(pairs_sent)
    everyone, others, own_head = pl.ds(0, T), pl.ds(1, T - 1), pl.ds(0, 1)
    near_moved = forward_pairs(pl.ds(0, 1), everyone, 0, near)
    others_moved = [forward_pairs(pl.ds(0, 1), others, 0, far)]
    for j in rest:
        backs[0][j] = send_back(0, j)
    arrive(rows_sent)
    arrive(part_sums[1])
    gather_projected(1, True)
    attend(1)
    pairs_sent = send_pairs(1)
    finish_queries(1)
    query_out = pltpu.make_async_copy(qg, qg_hbm, local_sem.at[2])
    query_out.start()
    arrive(near_moved[1])
    feature_grads(0, 2)
    features = [send_features(0, near)]
    arrive(pairs_sent)
    others_moved.append(forward_pairs(pl.ds(1, 1), others, 1))
    late_moved = [forward_pairs(pl.ds(1, 1), own_head, 2), forward_pairs(pl.ds(0, 1), own_head, 3, far)]
    for j in by_tensor[1]:
        backs[1][j] = send_back(1, j)

    for moved in others_moved:
        for j in moved:
            arrive(moved[j])
    arrive(columns_sent[1, 1])
    sums_sent = []
    for k in range(1, T):
        for h in range(2):
            here = pl.ds(h * HB, HB)
            accumulate(k, h)
            sums_sent += start([
                remote(sum_out.at[k - 1, here], sum_in.at[k - 1, here],
                       sum_s.at[k - 1, h], sum_r.at[k - 1, h], peer(T - k, 0))
            ])

    collect(0, backs[0], features[0])
    loads[4].wait()
    loads[5].wait()
    norm_back(0, lambda rows, here: sc[rows, here].astype(jnp.float32), outgoing)
    shift = start([remote(outgoing, incoming, out_s.at[0], out_r.at[0], down)])
    for moved in late_moved:
        for j in moved:
            arrive(moved[j])
    feature_grads(1, N)
    features.append(send_features(1, by_dp[1]))
    for h in range(2):
        accumulate(0, h)

    collect(1, backs[1], features[1])
    arrive(shift)
    is_last = section == S - 1

    def arriving(rows, here):
        return jnp.where(is_last, lc[rows, here].astype(jnp.float32), incoming[rows, here].astype(jnp.float32))

    norm_back(1, arriving, result)
    residual_out = pltpu.make_async_copy(result, rg_hbm, local_sem.at[0])
    residual_out.start()

    arrive(sums_sent)

    def finish(i, _):
        rows = pl.ds(pl.multiple_of(i * WR, WR), WR)
        final = sum_own[rows, :]
        for k in range(1, T):
            final = final + sum_in[k - 1, rows, :].astype(jnp.float32)
        pg[rows] = final.astype(jnp.bfloat16).reshape(WR, 2, HS)
        return _

    lax.fori_loop(0, BW // WR, finish, 0)
    weight_out = pltpu.make_async_copy(pg, pg_hbm, local_sem.at[1])
    weight_out.start()
    for copy in started:
        copy.wait_send()
    query_out.wait()
    residual_out.wait()
    weight_out.wait()


def copies(*refs):
    count = (len(refs) - 1) // 3
    sources, targets, held, sems = refs[:count], refs[count:2 * count], refs[2 * count:3 * count], refs[-1]
    moves = [
        [pltpu.make_async_copy(source, buffer, sems.at[i, 0]), pltpu.make_async_copy(buffer, target, sems.at[i, 1])]
        for i, (source, target, buffer) in enumerate(zip(sources, targets, held))
    ]
    for inward, _ in moves:
        inward.start()
    for inward, outward in moves:
        inward.wait()
        outward.start()
    for _, outward in moves:
        outward.wait()


def settle(arrays):
    anywhere = pl.BlockSpec(memory_space=pl.ANY)
    return pl.pallas_call(
        copies,
        out_shape=tuple(jax.ShapeDtypeStruct(array.shape, array.dtype) for array in arrays),
        in_specs=[anywhere] * len(arrays),
        out_specs=[anywhere] * len(arrays),
        scratch_shapes=[pltpu.VMEM(array.shape, array.dtype) for array in arrays] + [pltpu.SemaphoreType.DMA((len(arrays), 2))],
    )(*arrays)


def on_device(residuals, norm_gain, projection, queries, output_grad, section_cotangent, loss_cotangent, lengths, segments):
    x, q, og = residuals[0, 0], queries[0, 0, :, :, 0, :], output_grad[0, 0, :, :, 0, :]
    ticks, R, D = x.shape
    PW = 2 * projection.shape[4]
    S, T, N = (lax.axis_size(name) for name in ("section", "tensor", "dp"))
    TOK, BW, HB = R * T, D // N, D // N // 2
    sizes = (S, T, N, R, D, PW, q.shape[-1] // (PW // 2))
    low, wide, dma = jnp.bfloat16, jnp.float32, pltpu.SemaphoreType.DMA
    anywhere, vmem = pl.BlockSpec(memory_space=pl.ANY), pl.BlockSpec(memory_space=pltpu.VMEM)
    outs = pl.pallas_call(
        functools.partial(kernel, sizes),
        out_shape=(
            jax.ShapeDtypeStruct(q.shape, low),
            jax.ShapeDtypeStruct((R, D), low),
            jax.ShapeDtypeStruct((BW, 2, PW // 2), low),
        ),
        in_specs=[anywhere, vmem] + [anywhere] * 5 + [pl.BlockSpec(memory_space=pltpu.SMEM), vmem],
        out_specs=[anywhere] * 3,
        scratch_shapes=[
            pltpu.VMEM(x.shape, low), pltpu.VMEM((D, 2, PW // 2), low), pltpu.VMEM((D, PW), low), pltpu.VMEM(q.shape, low), pltpu.VMEM(q.shape, low),
            pltpu.VMEM((R, D), low), pltpu.VMEM((R, D), low),
            pltpu.VMEM((T - 1, BW, PW), low),
            pltpu.VMEM((ticks, N, 2, R, HB), low), pltpu.VMEM((ticks, R, 1), wide),
            pltpu.VMEM((ticks, 2, N, R, HB), low), pltpu.VMEM((T - 1, N, R, HB), low),
            pltpu.VMEM((ticks, N, T - 1, R, PW), low), pltpu.VMEM((ticks, N - 1, T - 1, R, PW), low),
            pltpu.VMEM((ticks, T - 1, R, PW), low), pltpu.VMEM((ticks, T - 1, R, PW), low),
            pltpu.VMEM((ticks, TOK, PW), low),
            pltpu.VMEM((ticks, TOK, PW), low), pltpu.VMEM((ticks, N, T, R, PW), low),
            pltpu.VMEM((ticks, N - 1, T, R, BW), low), pltpu.VMEM((ticks, N - 1, T - 1, R, BW), low),
            pltpu.VMEM((ticks, N - 1, R, BW), low), pltpu.VMEM((ticks, N - 1, R, BW), low), pltpu.VMEM((ticks, R, BW), wide),
            pltpu.VMEM((N, R, BW), wide),
            pltpu.VMEM((BW, PW), wide), pltpu.VMEM((T - 1, BW, PW), low), pltpu.VMEM((T - 1, BW, PW), low),
            pltpu.VMEM((R, D), low), pltpu.VMEM((R, D), low), pltpu.VMEM((R, D), low), pltpu.VMEM(q.shape, low),
            pltpu.VMEM((BW, 2, PW // 2), low),
            pltpu.VMEM((ticks, 2, TOK * q.shape[-1] // (PW // 2), PW // 2), low),
            pltpu.VMEM((ticks, TOK * q.shape[-1] // (PW // 2), TOK), low),
            dma((6,)), dma((N,)), dma((T - 1,)), dma((T - 1,)),
            dma((ticks, 2, N - 1)), dma((ticks, 2, N - 1)), dma((T - 1, 2)), dma((T - 1, 2)),
            dma((ticks, N - 1)), dma((ticks, N - 1)), dma((ticks, T - 1)), dma((ticks, T - 1)),
            dma((ticks, T - 1)), dma((ticks, T - 1)), dma((4, N - 1)), dma((4, N - 1)),
            dma((ticks, N - 1, T - 1)), dma((ticks, N - 1, T - 1)), dma((ticks, N - 1)), dma((ticks, N - 1)),
            dma((T - 1, 2)), dma((T - 1, 2)), dma((1,)), dma((1,)),
        ],
        compiler_params=pltpu.CompilerParams(
            collective_id=0, has_side_effects=True, vmem_limit_bytes=62_000_000
        ),
    )(
        x, norm_gain, projection.reshape(D, 2, PW // 2), q, og, section_cotangent[0, 0], loss_cotangent[0],
        lengths.reshape(ticks), segments[0, 0],
    )
    query_grad, residual_grad, projection_grad = settle(outs)
    return (
        query_grad[None, None, :, :, None, :],
        residual_grad[None, None],
        projection_grad.reshape(1, BW, 1, 2, PW // 2),
    )


def solution(mesh):
    in_specs = (
        P("section", "dp", None, "tensor", None),
        P("section", None),
        P("section", None, "tensor", None, None),
        P("section", "dp", None, None, "tensor", None),
        P("section", "dp", None, None, "tensor", None),
        P("section", "dp", "tensor", None),
        P("dp", "tensor", None),
        P("section", "dp", None),
        P("section", "dp", None, None),
    )
    out_specs = (
        P("section", "dp", None, None, "tensor", None),
        P("section", "dp", "tensor", None),
        P("section", "dp", "tensor", None, None),
    )
    return jax.shard_map(on_device, mesh=mesh, in_specs=in_specs, out_specs=out_specs, check_vma=False)
```

time: 112 us -> 98.8 us (0.88)
  local copies, waits for them, and re-layouts: 10.9 us -> 0 us
  Pallas kernels: 100 us -> 97.9 us
    unnamed x3 -> x0, local copies, waits for them, and re-layouts: 8.8 us -> none
    pallas_call x1, Pallas kernels: 100 us -> 95.2 us  [on_device(): pl.pallas_call(functools.partial(kernel, sizes), out_shape=(jax.ShapeDtyp...]
    pallas_call x0 -> x1, Pallas kernels: none -> 2.76 us  [settle(): pl.pallas_call(copies, out_shape=tuple((jax.ShapeDtypeStruct(array.shape,...]
    reshape x1 -> x0, local copies, waits for them, and re-layouts: 2.14 us -> none  [on_device(): projection_grad.reshape(1, BW, 1, 2, PW // 2)]
where the time goes in v1:
time: 98.8 us; the launch traced here: 98.6 us
  Pallas kernels  97.9 us (99%)
    pallas_call x1, Pallas kernels, on_device(): pl.pallas_call(functools.partial(kernel, sizes), out_shape=(jax.ShapeDtyp...  95.2 us
    pallas_call x1, Pallas kernels, settle(): pl.pallas_call(copies, out_shape=tuple((jax.ShapeDtypeStruct(array.shape,...  2.76 us

profile of v1, /device:TPU:0, one launch (start us, length us, event | category | flops | bytes accessed | tf_op | source)
XLA Modules:
  0.0 98.6 jit_solution(4144343578274281801)
XLA Ops:
  0.6 95.2 %shard_map.112 = (bf16[2,128,1024]{2,1,0:T(8,128)(2,1)}, bf16[64,8192]{1,0:T(8,128)(2,1)}, bf16[2048,2,128]{2,1,0:T(2,128)(2,1)}) custom-call(bf16[2,64,8192]{2,1,0:T(8,128)(2,1)} %bitcast.16, bf16[1,8192]{1,0:T(2,128)(2,1)} %gain_ref.1, bf16[8192,2,128]{2,1,0:T(2,128)(2,1)} %bitcast.15, bf16[2,128,1024]{2,1,0:T(8,128)(2,1)} %bitcast.19, ...), custom_call_target="tpu_custom_call" | custom-call | tf_op jit(solution)/shard_map/pallas_call | solution.py:473
  95.8 2.8 %shard_map.113 = (bf16[2,128,1024]{2,1,0:T(8,128)(2,1)}, bf16[64,8192]{1,0:T(8,128)(2,1)}, bf16[2048,2,128]{2,1,0:T(2,128)(2,1)}) custom-call(bf16[2,128,1024]{2,1,0:T(8,128)(2,1)} %get-tuple-element.9.refs_0_, bf16[64,8192]{1,0:T(8,128)(2,1)} %get-tuple-element.10.refs_1_, bf16[2048,2,128]{2,1,0:T(2,128)(2,1)} %get-tuple-element.11.refs_2_), custom_call_target="tpu_custom_call" | custom-call | tf_op jit(solution)/shard_map/pallas_call | solution.py:455

commit v2 on v1

--- a/solution.py
+++ b/solution.py
@@ -10,6 +10,8 @@
 EPSILON = 1e-05
 MASKED = -1e30
 ROWS = 16
+Q = 4
+FIRST = 1
 NT = (((1,), (1,)), ((), ()))
 TN = (((0,), (0,)), ((), ()))
 
@@ -31,7 +33,7 @@
     S, T, N, R, D, PW, G = sizes
     HS = PW // 2
     TOK, BW = R * T, D // N
-    HB = BW // 2
+    HB = BW // Q
     WR = min(BW, 256)
     section, me_t, me_n = (lax.axis_index(name) for name in ("section", "tensor", "dp"))
     scaling = HS ** (-0.5)
@@ -105,25 +107,25 @@
         def step(i, _):
             rows = pl.ds(pl.multiple_of(i * ROWS, ROWS), ROWS)
             squares = jnp.zeros((ROWS, HB), jnp.float32)
-            for p in range(2 * N):
+            for p in range(Q * N):
                 wide = x[tick, rows, p * HB:(p + 1) * HB].astype(jnp.float32)
                 squares = squares + wide * wide
             inverse = lax.rsqrt(jnp.sum(squares, axis=1, keepdims=True) / D + EPSILON)
             inv[tick, rows, :] = inverse
-            for p in range(2 * N):
+            for p in range(Q * N):
                 here = slice(p * HB, (p + 1) * HB)
                 wide = x[tick, rows, here].astype(jnp.float32)
                 gain = gain_ref[:, here].astype(jnp.float32)
-                nb[tick, p // 2, p % 2, rows, :] = (wide * inverse * gain).astype(jnp.bfloat16)
+                nb[tick, p // Q, p % Q, rows, :] = (wide * inverse * gain).astype(jnp.bfloat16)
             return _
         lax.fori_loop(0, R // ROWS, step, 0)
-        for h in range(2):
-            cols[tick, h, 0] = nb[tick, me_n, h]
-
-    def send_columns(tick, h, offsets=range(1, N)):
+        cols[tick, :, 0] = nb[tick, me_n]
+
+    def send_columns(tick, group, offsets=range(1, N)):
+        pieces = [pl.ds(0, FIRST), pl.ds(FIRST, Q - FIRST)][group]
         return start([
-            remote(nb.at[tick, block_at(j), h], cols.at[tick, h, j],
-                   col_s.at[tick, h, j - 1], col_r.at[tick, h, j - 1], peer(0, j))
+            remote(nb.at[tick, block_at(j), pieces], cols.at[tick, pieces, j],
+                   col_s.at[tick, group, j - 1], col_r.at[tick, group, j - 1], peer(0, j))
             for j in offsets
         ])
 
@@ -134,8 +136,8 @@
 
     def project_own(tick):
         value = jnp.zeros((R, PW), jnp.float32)
-        for p in range(2 * N):
-            value = value + dot(nb[tick, p // 2, p % 2], w[p * HB:(p + 1) * HB, :])
+        for p in range(Q * N):
+            value = value + dot(nb[tick, p // Q, p % Q], w[p * HB:(p + 1) * HB, :])
         proj[tick, own_tokens, :] = value.astype(jnp.bfloat16)
 
     def send_partials(tick, halves):
@@ -164,7 +166,7 @@
     def send_rows(piece):
         blocks = pl.ds(piece * (N // 2), N // 2)
         return start([
-            remote(nb.at[1, blocks, 1], rows_in.at[k - 1, blocks], row_s.at[k - 1, piece], row_r.at[k - 1, piece], peer(k, 0))
+            remote(nb.at[1, blocks, pl.ds(FIRST, Q - FIRST)], rows_in.at[k - 1, blocks], row_s.at[k - 1, piece], row_r.at[k - 1, piece], peer(k, 0))
             for k in range(1, T)
         ])
 
@@ -172,8 +174,9 @@
         for k in range(1, T):
             value = part_all[tick, k - 1].astype(jnp.float32)
             if cross:
-                for b in range(N):
-                    value = value + dot(rows_in[T - k - 1, b], w[b * BW + HB:(b + 1) * BW, :])
+                for p in range(N * Q):
+                    if p % Q >= FIRST:
+                        value = value + dot(rows_in[T - k - 1, p // Q, p % Q - FIRST], w[p * HB:(p + 1) * HB, :])
             proj[tick, tokens_of(k), :] = value.astype(jnp.bfloat16)
 
     position_q = lax.broadcasted_iota(jnp.int32, (TOK, TOK), 0)
@@ -330,10 +333,10 @@
         stack_heads(tick)
 
     arrive(weights_sent)
-    arrive(columns_sent[0, 0])
-    arrive(columns_sent[0, 1])
+    for group in range(2):
+        arrive(columns_sent[0, group])
     near, far = range(1, 2), range(2, N)
-    partials = send_partials(0, (0, 1))
+    partials = send_partials(0, range(Q))
     columns_sent[1, 0] = send_columns(1, 0, near)
     columns_sent[1, 0] = columns_sent[1, 0] + send_columns(1, 0, far)
     arrive(partials)
@@ -347,7 +350,7 @@
     first, *rest = by_tensor[0]
     backs[0][first] = send_back(0, first)
     arrive(columns_sent[1, 0])
-    partials = send_partials(1, (0,))
+    partials = send_partials(1, range(FIRST))
     columns_sent[1, 1] = send_columns(1, 1, near)
     columns_sent[1, 1] = columns_sent[1, 1] + send_columns(1, 1, far)
     finish_queries(0)
@@ -364,17 +367,17 @@
     gather_projected(1, True)
     attend(1)
     pairs_sent = send_pairs(1)
+    arrive(pairs_sent)
+    others_moved.append(forward_pairs(pl.ds(1, 1), others, 1))
+    arrive(near_moved[1])
+    feature_grads(0, 2)
+    features = [send_features(0, near)]
+    late_moved = [forward_pairs(pl.ds(1, 1), own_head, 2), forward_pairs(pl.ds(0, 1), own_head, 3, far)]
+    for j in by_tensor[1]:
+        backs[1][j] = send_back(1, j)
     finish_queries(1)
     query_out = pltpu.make_async_copy(qg, qg_hbm, local_sem.at[2])
     query_out.start()
-    arrive(near_moved[1])
-    feature_grads(0, 2)
-    features = [send_features(0, near)]
-    arrive(pairs_sent)
-    others_moved.append(forward_pairs(pl.ds(1, 1), others, 1))
-    late_moved = [forward_pairs(pl.ds(1, 1), own_head, 2), forward_pairs(pl.ds(0, 1), own_head, 3, far)]
-    for j in by_tensor[1]:
-        backs[1][j] = send_back(1, j)
 
     for moved in others_moved:
         for j in moved:
@@ -382,7 +385,7 @@
     arrive(columns_sent[1, 1])
     sums_sent = []
     for k in range(1, T):
-        for h in range(2):
+        for h in range(Q):
             here = pl.ds(h * HB, HB)
             accumulate(k, h)
             sums_sent += start([
@@ -400,7 +403,7 @@
             arrive(moved[j])
     feature_grads(1, N)
     features.append(send_features(1, by_dp[1]))
-    for h in range(2):
+    for h in range(Q):
         accumulate(0, h)
 
     collect(1, backs[1], features[1])
@@ -466,7 +469,7 @@
     ticks, R, D = x.shape
     PW = 2 * projection.shape[4]
     S, T, N = (lax.axis_size(name) for name in ("section", "tensor", "dp"))
-    TOK, BW, HB = R * T, D // N, D // N // 2
+    TOK, BW, HB = R * T, D // N, D // N // Q
     sizes = (S, T, N, R, D, PW, q.shape[-1] // (PW // 2))
     low, wide, dma = jnp.bfloat16, jnp.float32, pltpu.SemaphoreType.DMA
     anywhere, vmem = pl.BlockSpec(memory_space=pl.ANY), pl.BlockSpec(memory_space=pltpu.VMEM)
@@ -483,8 +486,8 @@
             pltpu.VMEM(x.shape, low), pltpu.VMEM((D, 2, PW // 2), low), pltpu.VMEM((D, PW), low), pltpu.VMEM(q.shape, low), pltpu.VMEM(q.shape, low),
             pltpu.VMEM((R, D), low), pltpu.VMEM((R, D), low),
             pltpu.VMEM((T - 1, BW, PW), low),
-            pltpu.VMEM((ticks, N, 2, R, HB), low), pltpu.VMEM((ticks, R, 1), wide),
-            pltpu.VMEM((ticks, 2, N, R, HB), low), pltpu.VMEM((T - 1, N, R, HB), low),
+            pltpu.VMEM((ticks, N, Q, R, HB), low), pltpu.VMEM((ticks, R, 1), wide),
+            pltpu.VMEM((ticks, Q, N, R, HB), low), pltpu.VMEM((T - 1, N, Q - FIRST, R, HB), low),
             pltpu.VMEM((ticks, N, T - 1, R, PW), low), pltpu.VMEM((ticks, N - 1, T - 1, R, PW), low),
             pltpu.VMEM((ticks, T - 1, R, PW), low), pltpu.VMEM((ticks, T - 1, R, PW), low),
             pltpu.VMEM((ticks, TOK, PW), low),
@@ -502,7 +505,7 @@
             dma((ticks, N - 1)), dma((ticks, N - 1)), dma((ticks, T - 1)), dma((ticks, T - 1)),
             dma((ticks, T - 1)), dma((ticks, T - 1)), dma((4, N - 1)), dma((4, N - 1)),
             dma((ticks, N - 1, T - 1)), dma((ticks, N - 1, T - 1)), dma((ticks, N - 1)), dma((ticks, N - 1)),
-            dma((T - 1, 2)), dma((T - 1, 2)), dma((1,)), dma((1,)),
+            dma((T - 1, Q)), dma((T - 1, Q)), dma((1,)), dma((1,)),
         ],
         compiler_params=pltpu.CompilerParams(
             collective_id=0, has_side_effects=True, vmem_limit_bytes=62_000_000

time: 98.8 us -> 97.1 us (0.983)
  Pallas kernels: 97.9 us -> 96.3 us
    pallas_call x1, Pallas kernels: 95.2 us -> 93.5 us  [on_device(): pl.pallas_call(functools.partial(kernel, sizes), out_shape=(jax.ShapeDtyp...]
where the time goes in v2:
time: 97.1 us; the launch traced here: 96.9 us
  Pallas kernels  96.3 us (99%)
    pallas_call x1, Pallas kernels, on_device(): pl.pallas_call(functools.partial(kernel, sizes), out_shape=(jax.ShapeDtyp...  93.5 us
    pallas_call x1, Pallas kernels, settle(): pl.pallas_call(copies, out_shape=tuple((jax.ShapeDtypeStruct(array.shape,...  2.76 us

profile of v2, /device:TPU:0, one launch (start us, length us, event | category | flops | bytes accessed | tf_op | source)
XLA Modules:
  0.0 96.9 jit_solution(13879858762415503532)
XLA Ops:
  0.6 93.5 %shard_map.112 = (bf16[2,128,1024]{2,1,0:T(8,128)(2,1)}, bf16[64,8192]{1,0:T(8,128)(2,1)}, bf16[2048,2,128]{2,1,0:T(2,128)(2,1)}) custom-call(bf16[2,64,8192]{2,1,0:T(8,128)(2,1)} %bitcast.16, bf16[1,8192]{1,0:T(2,128)(2,1)} %gain_ref.1, bf16[8192,2,128]{2,1,0:T(2,128)(2,1)} %bitcast.15, bf16[2,128,1024]{2,1,0:T(8,128)(2,1)} %bitcast.19, ...), custom_call_target="tpu_custom_call" | custom-call | tf_op jit(solution)/shard_map/pallas_call | solution.py:476
  94.2 2.8 %shard_map.113 = (bf16[2,128,1024]{2,1,0:T(8,128)(2,1)}, bf16[64,8192]{1,0:T(8,128)(2,1)}, bf16[2048,2,128]{2,1,0:T(2,128)(2,1)}) custom-call(bf16[2,128,1024]{2,1,0:T(8,128)(2,1)} %get-tuple-element.9.refs_0_, bf16[64,8192]{1,0:T(8,128)(2,1)} %get-tuple-element.10.refs_1_, bf16[2048,2,128]{2,1,0:T(2,128)(2,1)} %get-tuple-element.11.refs_2_), custom_call_target="tpu_custom_call" | custom-call | tf_op jit(solution)/shard_map/pallas_call | solution.py:458

commit v3 on v2

--- a/solution.py
+++ b/solution.py
@@ -73,8 +73,6 @@
         for copy in copies:
             copy.wait_recv()
 
-    own_rows = pl.ds(pl.multiple_of(me_n * BW, BW), BW)
-
     def weight_rows(j):
         return pl.ds(pl.multiple_of(block_at(j) * BW, BW), BW)
 
@@ -93,15 +91,16 @@
     for device in greet:
         pl.semaphore_signal(barrier, 1, device_id=device, device_id_type=pl.DeviceIdType.MESH)
 
-    def place_weights(j):
-        raw_loads[j].wait()
-        first = block_at(j) * BW
+    def place_weights(j, part=0, parts=1):
+        if part == 0:
+            raw_loads[j].wait()
+        first = block_at(j) * BW + part * (BW // parts)
 
         def step(i, _):
             rows = pl.ds(pl.multiple_of(first + i * WR, WR), WR)
             w[rows, :] = raw[rows].reshape(WR, PW)
             return _
-        lax.fori_loop(0, BW // WR, step, 0)
+        lax.fori_loop(0, BW // parts // WR, step, 0)
 
     def normalize(tick):
         def step(i, _):
@@ -316,10 +315,15 @@
     normalize(0)
     pl.semaphore_wait(barrier, len(greet))
     columns_sent = {(0, h): send_columns(0, h) for h in range(2)}
-    place_weights(0)
-    weights_sent = start([
-        remote(w.at[own_rows], wo.at[k - 1], wo_s.at[k - 1], wo_r.at[k - 1], peer(k, 0)) for k in range(1, T)
-    ])
+    weights_sent = []
+    for part in range(2):
+        place_weights(0, part, 2)
+        rows = pl.ds(pl.multiple_of(me_n * BW + part * (BW // 2), BW // 2), BW // 2)
+        weights_sent += start([
+            remote(w.at[rows], wo.at[k - 1, pl.ds(part * (BW // 2), BW // 2)],
+                   wo_s.at[k - 1, part], wo_r.at[k - 1, part], peer(k, 0))
+            for k in range(1, T)
+        ])
     loads[1].wait()
     normalize(1)
     rows_sent = send_rows(0)
@@ -440,10 +444,16 @@
 def copies(*refs):
     count = (len(refs) - 1) // 3
     sources, targets, held, sems = refs[:count], refs[count:2 * count], refs[2 * count:3 * count], refs[-1]
-    moves = [
-        [pltpu.make_async_copy(source, buffer, sems.at[i, 0]), pltpu.make_async_copy(buffer, target, sems.at[i, 1])]
-        for i, (source, target, buffer) in enumerate(zip(sources, targets, held))
-    ]
+    moves = []
+    for i, (source, target, buffer) in enumerate(zip(sources, targets, held)):
+        pieces = min(4, source.shape[0] // ROWS) or source.shape[0]
+        size = source.shape[0] // pieces
+        for p in range(pieces):
+            rows = pl.ds(p * size, size)
+            moves.append((
+                pltpu.make_async_copy(source.at[rows], buffer.at[rows], sems.at[i, p, 0]),
+                pltpu.make_async_copy(buffer.at[rows], target.at[rows], sems.at[i, p, 1]),
+            ))
     for inward, _ in moves:
         inward.start()
     for inward, outward in moves:
@@ -460,7 +470,8 @@
         out_shape=tuple(jax.ShapeDtypeStruct(array.shape, array.dtype) for array in arrays),
         in_specs=[anywhere] * len(arrays),
         out_specs=[anywhere] * len(arrays),
-        scratch_shapes=[pltpu.VMEM(array.shape, array.dtype) for array in arrays] + [pltpu.SemaphoreType.DMA((len(arrays), 2))],
+        scratch_shapes=[pltpu.VMEM(array.shape, array.dtype) for array in arrays]
+        + [pltpu.SemaphoreType.DMA((len(arrays), 4, 2))],
     )(*arrays)
 
 
@@ -500,7 +511,7 @@
             pltpu.VMEM((BW, 2, PW // 2), low),
             pltpu.VMEM((ticks, 2, TOK * q.shape[-1] // (PW // 2), PW // 2), low),
             pltpu.VMEM((ticks, TOK * q.shape[-1] // (PW // 2), TOK), low),
-            dma((6,)), dma((N,)), dma((T - 1,)), dma((T - 1,)),
+            dma((6,)), dma((N,)), dma((T - 1, 2)), dma((T - 1, 2)),
             dma((ticks, 2, N - 1)), dma((ticks, 2, N - 1)), dma((T - 1, 2)), dma((T - 1, 2)),
             dma((ticks, N - 1)), dma((ticks, N - 1)), dma((ticks, T - 1)), dma((ticks, T - 1)),
             dma((ticks, T - 1)), dma((ticks, T - 1)), dma((4, N - 1)), dma((4, N - 1)),

time: 97.1 us -> 96.5 us (level)
  no operation moved by 1% of the time
where the time goes in v3:
time: 96.5 us; the launch traced here: 96.3 us
  Pallas kernels  95.7 us (99%)
    pallas_call x1, Pallas kernels, on_device(): pl.pallas_call(functools.partial(kernel, sizes), out_shape=(jax.ShapeDtyp...  93 us
    pallas_call x1, Pallas kernels, settle(): pl.pallas_call(copies, out_shape=tuple((jax.ShapeDtypeStruct(array.shape,...  2.64 us

profile of v3, /device:TPU:0, one launch (start us, length us, event | category | flops | bytes accessed | tf_op | source)
XLA Modules:
  0.0 96.3 jit_solution(14922791673083107731)
XLA Ops:
  0.6 93.0 %shard_map.112 = (bf16[2,128,1024]{2,1,0:T(8,128)(2,1)}, bf16[64,8192]{1,0:T(8,128)(2,1)}, bf16[2048,2,128]{2,1,0:T(2,128)(2,1)}) custom-call(bf16[2,64,8192]{2,1,0:T(8,128)(2,1)} %bitcast.16, bf16[1,8192]{1,0:T(2,128)(2,1)} %gain_ref.1, bf16[8192,2,128]{2,1,0:T(2,128)(2,1)} %bitcast.15, bf16[2,128,1024]{2,1,0:T(8,128)(2,1)} %bitcast.19, ...), custom_call_target="tpu_custom_call" | custom-call | tf_op jit(solution)/shard_map/pallas_call | solution.py:487
  93.7 2.6 %shard_map.113 = (bf16[2,128,1024]{2,1,0:T(8,128)(2,1)}, bf16[64,8192]{1,0:T(8,128)(2,1)}, bf16[2048,2,128]{2,1,0:T(2,128)(2,1)}) custom-call(bf16[2,128,1024]{2,1,0:T(8,128)(2,1)} %get-tuple-element.9.refs_0_, bf16[64,8192]{1,0:T(8,128)(2,1)} %get-tuple-element.10.refs_1_, bf16[2048,2,128]{2,1,0:T(2,128)(2,1)} %get-tuple-element.11.refs_2_), custom_call_target="tpu_custom_call" | custom-call | tf_op jit(solution)/shard_map/pallas_call | solution.py:468
